TPU v7x, 32 devices: a whole 2x2x4 slice. The times are simulated.
32 devices in a mesh: tm: 8 (over z, core), dp: 4 (over y, x).
Axes of the slice: x: 2, y: 2, z: 4, core: 2. Of those that a mesh axis runs over, the one named last changes fastest.
Arguments:
- encoded: bfloat16 [512, 80, 1024], P('dp', 'tm'), may hold values from -6 to 6
- queries: bfloat16 [512, 32, 1024], P(('dp', 'tm')), may hold values from -200 to 200
- cotangent: bfloat16 [512, 32, 1024], P(('dp', 'tm')), may hold values from -0.08886719 to 0.08886719
- lengths: int32 [512], P(('dp', 'tm')), may hold values from 2 to 80
- key_weight: bfloat16 [1024, 1024], replicated, may hold values from -0.1875 to 0.1875
- value_weight: bfloat16 [1024, 1024], replicated, may hold values from -0.1875 to 0.1875
Outputs:
- context: bfloat16 [512, 32, 1024], P(('dp', 'tm'))
- key_grad: float32 [1024, 1024], replicated
- value_grad: float32 [1024, 1024], replicated
Inputs may be any that keep to these rules, and one draw needn't show every extreme that they name: Sequence b attends only to source positions below lengths[b].
All inputs are finite; a program needn't handle non-finite values.
Results may differ from a plain program's by a relative error of at most 0.0069.
Values may be sent and summed in bfloat16 or wider, within the bound.
A program may use at most 128 MiB of HBM per device.

v0:
```python
import math
import jax
import jax.numpy as jnp
from jax import lax
from jax.sharding import PartitionSpec as P


def attend(queries, key_rows, value_rows, lengths, cotangent):
    score_scale = 1.0 / math.sqrt(queries.shape[-1])
    scores = (
        jnp.einsum("btd,bsd->bts", queries, key_rows, preferred_element_type=jnp.float32)
        * score_scale
    )
    positions = jnp.arange(key_rows.shape[1], dtype=jnp.int32)
    in_range = positions[None, None, :] < lengths[:, None, None]
    scores = jnp.where(in_range, scores, -1e30)
    row_max = jnp.max(scores, axis=-1, keepdims=True)
    weights = jnp.exp(scores - row_max)
    probabilities = weights / jnp.sum(weights, axis=-1, keepdims=True)
    probs_low = probabilities.astype(jnp.bfloat16)
    context = jnp.einsum(
        "bts,bsd->btd", probs_low, value_rows, preferred_element_type=jnp.float32
    ).astype(jnp.bfloat16)
    grad_probs = jnp.einsum(
        "btd,bsd->bts", cotangent, value_rows, preferred_element_type=jnp.float32
    )
    grad_scores = probabilities * (
        grad_probs - jnp.sum(probabilities * grad_probs, axis=-1, keepdims=True)
    )
    grad_low = grad_scores.astype(jnp.bfloat16)
    grad_values = jnp.einsum(
        "bts,btd->bsd", probs_low, cotangent, preferred_element_type=jnp.float32
    ).astype(jnp.bfloat16)
    grad_keys = (
        jnp.einsum("bts,btd->bsd", grad_low, queries, preferred_element_type=jnp.float32)
        * score_scale
    ).astype(jnp.bfloat16)
    return (context, grad_keys, grad_values)


def project(flattened, weight_matrix, shape):
    return (
        jnp.dot(flattened, weight_matrix, preferred_element_type=jnp.float32)
        .astype(jnp.bfloat16)
        .reshape(shape)
    )


def weight_term(flattened, gradient):
    model_width = flattened.shape[1]
    return lax.dot_general(
        flattened,
        gradient.reshape(-1, model_width),
        (((0,), (0,)), ((), ())),
        preferred_element_type=jnp.float32,
    )


def body(encoded, queries, cotangent, lengths, key_weight, value_weight):
    model_width = encoded.shape[2]
    regrouped = lax.all_to_all(encoded, "tm", split_axis=0, concat_axis=1, tiled=True)
    flattened = regrouped.reshape(-1, model_width)
    key_rows = project(flattened, key_weight, regrouped.shape)
    value_rows = project(flattened, value_weight, regrouped.shape)
    context, grad_keys, grad_values = attend(queries, key_rows, value_rows, lengths, cotangent)
    key_grad = weight_term(flattened, grad_keys)
    value_grad = weight_term(flattened, grad_values)
    key_grad, value_grad = lax.psum((key_grad, value_grad), ("tm", "dp"))
    return (context, key_grad, value_grad)


def solution(mesh):
    return jax.shard_map(
        body,
        mesh=mesh,
        in_specs=(
            P("dp", "tm", None),
            P(("dp", "tm"), None, None),
            P(("dp", "tm"), None, None),
            P(("dp", "tm")),
            P(),
            P(),
        ),
        out_specs=(P(("dp", "tm"), None, None), P(), P()),
        check_vma=False,
    )
```

profile of v0, /device:TPU:0, one launch (start us, length us, event | category | flops | bytes accessed | tf_op | source)
XLA Modules:
  0.0 355.5 jit_solution(7292842336370048144)
XLA Ops:
  7.2 0.0 copy-start
  7.2 5.5 %copy.14 = bf16[128,10,1024]{2,1,0:T(8,128)(2,1)} copy(bf16[128,10,1024]{2,0,1:T(8,128)(2,1)} %param.6) | data formatting | bytes 5242880 | tf_op args[0]
  12.7 0.0 copy-start.5
  12.7 6.5 %all-to-all-start = ((bf16[128,10,1024]{2,1,0:T(8,128)(2,1)}), bf16[128,10,1024]{2,1,0:T(8,128)(2,1)}, u32[]{:S(2)}, u32[]{:S(2)}) async-start(bf16[128,10,1024]{2,1,0:T(8,128)(2,1)} %copy.14), calls=%async_computation | async-start | bytes 8388608 | tf_op jit(solution)/shard_map/all_to_all | solution.py:61
  19.2 0.0 all-reduce.3.cloned.1.call-start
  19.2 0.0 copy-done.5
  19.3 0.1 iota_compare_fusion
  19.3 94.0 %all-to-all-done = bf16[128,10,1024]{2,1,0:T(8,128)(2,1)} async-done(((bf16[128,10,1024]{2,1,0:T(8,128)(2,1)}), bf16[128,10,1024]{2,1,0:T(8,128)(2,1)}, u32[]{:S(2)}, u32[]{:S(2)}) %all-to-all-start) | async-done | bytes 2621472 | tf_op jit(solution)/shard_map/all_to_all | solution.py:61
  113.3 5.0 %copy.19 = bf16[8,16,10,1024]{3,2,0,1:T(8,128)(2,1)} copy(bf16[8,16,10,1024]{3,2,1,0:T(8,128)(2,1)} %bitcast) | data formatting | bytes 5242880 | tf_op jit(solution)/shard_map/all_to_all | solution.py:61
  118.3 6.1 %reshape.46 = bf16[1280,1024]{1,0:T(8,128)(2,1)} reshape(bf16[16,8,10,1024]{3,2,1,0:T(8,128)(2,1)} %bitcast.35) | data formatting | bytes 5242880 | tf_op jit(solution)/shard_map/reshape | solution.py:62
  124.5 0.0 copy-done
  124.5 0.0 copy-start.3
  124.5 0.0 copy-start.6
  124.5 6.1 %convolution_convert_fusion = bf16[1280,1024]{1,0:T(8,128)(2,1)} fusion(bf16[1280,1024]{1,0:T(8,128)(2,1)} %reshape.46, bf16[1024,1024]{1,0:T(8,128)(2,1)S(1)} %copy-done), kind=kOutput, calls=%fused_computation.3 | convolution fusion | flops 2685665280 | bytes 7340032 | tf_op jit(solution)/shard_map/dot_general | solution.py:43
  130.6 0.0 copy-done.3
  130.6 0.0 copy-done.6
  130.6 3.1 convolution_convert_fusion.1
  133.7 0.0 copy-done.1
  133.7 0.8 fusion.4
  134.6 0.9 fusion.8
  135.4 4.6 %convolution_convert_fusion.2 = bf16[16,80,1024]{2,1,0:T(8,128)(2,1)} fusion(bf16[16,32,1024]{2,1,0:T(8,128)(2,1)} %param.8, f32[16,32]{1,0:T(8,128)S(1)} %get-tuple-element.14, f32[16,32,80]{2,1,0:T(8,128)S(1)} %fusion.4), kind=kOutput, calls=%fused_computation.7 | convolution fusion | flops 85320272 | bytes 3835904 | tf_op jit(solution)/shard_map/bts,btd->bsd/dot_general | solution.py:31
  140.0 3.6 %multiply_reduce_fusion = (f32[16,32]{1,0:T(8,128)S(1)}, f32[16,32,80]{2,1,0:T(8,128)}) fusion(f32[16,32,80]{2,1,0:T(8,128)} %get-tuple-element.15, f32[16,32]{1,0:T(8,128)S(1)} %get-tuple-element.14, bf16[16,80,1024]{2,1,0:T(8,128)(2,1)} %bitcast.36, bf16[16,32,1024]{2,1,0:T(8,128)(2,1)} %param.8), kind=kOutput, calls=%fused_computation.16 | convolution fusion | flops 84008448 | bytes 4001792 | tf_op jit(solution)/shard_map/btd,bsd->bts/dot_general | solution.py:24
  143.6 4.1 %multiply_convert_fusion = bf16[16,80,1024]{2,1,0:T(8,128)(2,1)} fusion(bf16[16,32,1024]{2,1,0:T(8,128)(2,1)S(1)} %copy-done.1, f32[16,32,80]{2,1,0:T(8,128)} %get-tuple-element.17, f32[16,32]{1,0:T(8,128)S(1)} %get-tuple-element.16, f32[16,32]{1,0:T(8,128)S(1)} %get-tuple-element.14, f32[16,32,80]{2,1,0:T(8,128)S(1)} %fusion.4), kind=kOutput, calls=%fused_computation.1 | convolution fusion | flops 86712912 | bytes 4001792 | tf_op jit(solution)/shard_map/bts,btd->bsd/dot_general | solution.py:35
  147.8 7.6 %convolution_bitcast_fusion.1 = f32[1024,1024]{0,1:T(8,128)} fusion(bf16[1280,1024]{1,0:T(8,128)(2,1)} %bitcast.40, bf16[1280,1024]{1,0:T(8,128)(2,1)} %reshape.46), kind=kOutput, calls=%fused_computation.6 | convolution fusion | flops 2684354560 | bytes 9437184 | tf_op jit(solution)/shard_map/dot_general | solution.py:51
  155.4 0.0 copy-done.2
  155.4 0.0 copy-done.4
  155.4 4.4 %convolution_bitcast_fusion = f32[1024,1024]{0,1:T(8,128)} fusion(bf16[1280,1024]{1,0:T(8,128)(2,1)S(1)} %bitcast.38, bf16[1280,1024]{1,0:T(8,128)(2,1)S(1)} %copy-done.4), kind=kOutput, calls=%fused_computation.5 | convolution fusion | flops 2684354560 | bytes 9437184 | tf_op jit(solution)/shard_map/dot_general | solution.py:51
  159.8 0.0 all-reduce.3.cloned.1.call-update
  159.9 3.8 %convolution_convert_fusion.3 = bf16[16,32,1024]{2,1,0:T(8,128)(2,1)} fusion(bf16[16,80,1024]{2,1,0:T(8,128)(2,1)} %bitcast.37, f32[16,32]{1,0:T(8,128)S(1)} %get-tuple-element.14, f32[16,32,80]{2,1,0:T(8,128)S(1)} %fusion.4), kind=kOutput, calls=%fused_computation.8 | convolution fusion | flops 84533840 | bytes 3835904 | tf_op jit(solution)/shard_map/bts,bsd->btd/dot_general | solution.py:21
  163.7 174.3 %all-reduce.3.cloned.1.call-done = (f32[1024,1024]{0,1:T(8,128)}, f32[1024,1024]{0,1:T(8,128)}) async-done(((f32[1024,1024]{0,1:T(8,128)}, f32[1024,1024]{0,1:T(8,128)}), (f32[1024,1024]{0,1:T(8,128)}, f32[1024,1024]{0,1:T(8,128)})) %all-reduce.3.cloned.1.call-update) | async-done | bytes 8388624 | tf_op jit(solution)/shard_map/psum | solution.py:68
  338.0 5.3 %copy.16 = f32[1024,1024]{1,0:T(8,128)} copy(f32[1024,1024]{0,1:T(8,128)} %get-tuple-element.12) | data formatting | bytes 8388608
  343.4 5.3 %copy.17 = f32[1024,1024]{1,0:T(8,128)} copy(f32[1024,1024]{0,1:T(8,128)} %get-tuple-element.13) | data formatting | bytes 8388608
  (3 shorter events, 0.0 us)
Async XLA Ops:
  7.2 117.3 %copy-start = (bf16[1024,1024]{1,0:T(8,128)(2,1)S(1)}, bf16[1024,1024]{1,0:T(8,128)(2,1)}, u32[]{:S(2)}) copy-start(bf16[1024,1024]{1,0:T(8,128)(2,1)} %param.11) | copy-start | bytes 6291460
  12.7 6.5 %copy-start.5 = (s32[16]{0:T(128)S(1)}, s32[16]{0:T(128)}, u32[]{:S(2)}) copy-start(s32[16]{0:T(128)} %param.9) | copy-start | bytes 196
  12.7 100.6 %all-to-all-start = ((bf16[128,10,1024]{2,1,0:T(8,128)(2,1)}), bf16[128,10,1024]{2,1,0:T(8,128)(2,1)}, u32[]{:S(2)}, u32[]{:S(2)}) async-start(bf16[128,10,1024]{2,1,0:T(8,128)(2,1)} %copy.14), calls=%async_computation | async-start | bytes 8388608 | tf_op jit(solution)/shard_map/all_to_all | solution.py:61
  19.2 318.8 %all-reduce.3.cloned.1.call-start = ((), (), s32[]{:S(2)}) async-start(), calls=%async_computation.1 | async-start | bytes 16777216 | tf_op jit(solution)/shard_map/psum | solution.py:68
  124.5 6.1 %copy-start.3 = (bf16[1280,1024]{1,0:T(8,128)(2,1)S(1)}, bf16[1280,1024]{1,0:T(8,128)(2,1)}, u32[]{:S(2)}) copy-start(bf16[1280,1024]{1,0:T(8,128)(2,1)} %reshape.46) | copy-start | bytes 7864324
  124.5 6.1 %copy-start.6 = (bf16[1024,1024]{1,0:T(8,128)(2,1)S(1)}, bf16[1024,1024]{1,0:T(8,128)(2,1)}, u32[]{:S(2)}) copy-start(bf16[1024,1024]{1,0:T(8,128)(2,1)} %param.10) | copy-start | bytes 6291460
  130.6 3.1 copy-start.1
  147.8 7.6 %copy-start.2 = (bf16[16,80,1024]{2,1,0:T(8,128)(2,1)S(1)}, bf16[16,80,1024]{2,1,0:T(8,128)(2,1)}, u32[]{:S(2)}) copy-start(bf16[16,80,1024]{2,1,0:T(8,128)(2,1)} %convolution_convert_fusion.2) | copy-start | bytes 7864324
  147.8 7.6 %copy-start.4 = (bf16[1280,1024]{1,0:T(8,128)(2,1)S(1)}, bf16[1280,1024]{1,0:T(8,128)(2,1)}, u32[]{:S(2)}) copy-start(bf16[1280,1024]{1,0:T(8,128)(2,1)} %reshape.46) | copy-start | bytes 7864324
Sparse Core Ops, SparseCore 0:
  160.0 177.9 all-reduce.2
where the time goes:
time: 356 us
  waiting for transfers between devices  268 us (75%)
  matrix products  38.3 us (11%)
  local copies, waits for them, and re-layouts  27.4 us (8%)
  between operations  14.1 us (4%)
  starting transfers between devices  6.52 us (2%)
    psum x1, waiting for transfers between devices, body(): key_grad, value_grad = lax.psum((key_grad, value_grad), ('tm', 'dp'))  174 us
    all_to_all x1, waiting for transfers between devices, body(): lax.all_to_all(encoded, 'tm', split_axis=0, concat_axis=1, tiled=True)  94 us
    unnamed x17, local copies, waits for them, and re-layouts  16.2 us
    dot_general x2, matrix products, weight_term(): lax.dot_general(flattened, gradient.reshape(-1, model_width), (((0,), (0,...  12.1 us
    dot_general x2, matrix products, project(): jnp.dot(flattened, weight_matrix, preferred_element_type=jnp.float32)  9.23 us
  transfers between devices with their start and end apart: 2, of which 2 were waited for; matrix products, arithmetic and copies ran while one was open for 1% of the time, Pallas kernels for 0%

commit v1 on v0

--- a/solution.py
+++ b/solution.py
@@ -65,7 +65,7 @@
     context, grad_keys, grad_values = attend(queries, key_rows, value_rows, lengths, cotangent)
     key_grad = weight_term(flattened, grad_keys)
     value_grad = weight_term(flattened, grad_values)
-    key_grad, value_grad = lax.psum((key_grad, value_grad), ("tm", "dp"))
+    key_grad, value_grad = lax.psum(lax.psum((key_grad, value_grad), "tm"), "dp")
     return (context, key_grad, value_grad)
 
 

time: 356 us -> 527 us (1.48)
  waiting for transfers between devices: 268 us -> 441 us
    psum x1 -> x2, waiting for transfers between devices: 174 us -> 347 us  [the longest x1 175 us: body(): lax.psum((key_grad, value_grad), 'tm')]
    unnamed x17 -> x21, local copies, waits for them, and re-layouts: 16.2 us -> 16.4 us
  transfers between devices with their start and end apart: 2 -> 3, of which waited for: 2 -> 3; matrix products, arithmetic and copies ran while one was open for 1% -> 1% of each run, Pallas kernels for 0% -> 0%
where the time goes in v1:
time: 527 us
  waiting for transfers between devices  441 us (84%)
  matrix products  35.2 us (7%)
  local copies, waits for them, and re-layouts  27.6 us (5%)
  between operations  14.1 us (3%)
  starting transfers between devices  6.56 us (1%)
    psum x1, waiting for transfers between devices, body(): lax.psum((key_grad, value_grad), 'tm')  175 us
    psum x1, waiting for transfers between devices, body(): lax.psum(lax.psum((key_grad, value_grad), 'tm'), 'dp')  172 us
    all_to_all x1, waiting for transfers between devices, body(): lax.all_to_all(encoded, 'tm', split_axis=0, concat_axis=1, tiled=True)  94 us
    unnamed x21, local copies, waits for them, and re-layouts  16.4 us
    dot_general x2, matrix products, weight_term(): lax.dot_general(flattened, gradient.reshape(-1, model_width), (((0,), (0,...  12.1 us
  transfers between devices with their start and end apart: 3, of which 3 were waited for; matrix products, arithmetic and copies ran while one was open for 1% of the time, Pallas kernels for 0%

profile of v1, /device:TPU:0, one launch (start us, length us, event | category | flops | bytes accessed | tf_op | source)
XLA Modules:
  0.0 526.9 jit_solution(4211572156688250473)
XLA Ops:
  7.2 0.0 copy-start
  7.2 5.5 %copy.14 = bf16[128,10,1024]{2,1,0:T(8,128)(2,1)} copy(bf16[128,10,1024]{2,0,1:T(8,128)(2,1)} %param.6) | data formatting | bytes 5242880 | tf_op args[0]
  12.7 6.5 %all-to-all-start = ((bf16[128,10,1024]{2,1,0:T(8,128)(2,1)}), bf16[128,10,1024]{2,1,0:T(8,128)(2,1)}, u32[]{:S(2)}, u32[]{:S(2)}) async-start(bf16[128,10,1024]{2,1,0:T(8,128)(2,1)} %copy.14), calls=%async_computation | async-start | bytes 8388608 | tf_op jit(solution)/shard_map/all_to_all | solution.py:61
  19.2 0.0 all-reduce.5.cloned.1.call-start
  19.2 0.0 copy-done.7
  19.3 0.1 iota_compare_fusion
  19.3 94.0 %all-to-all-done = bf16[128,10,1024]{2,1,0:T(8,128)(2,1)} async-done(((bf16[128,10,1024]{2,1,0:T(8,128)(2,1)}), bf16[128,10,1024]{2,1,0:T(8,128)(2,1)}, u32[]{:S(2)}, u32[]{:S(2)}) %all-to-all-start) | async-done | bytes 2621472 | tf_op jit(solution)/shard_map/all_to_all | solution.py:61
  113.3 5.0 copy.19
  118.3 6.1 %reshape.46 = bf16[1280,1024]{1,0:T(8,128)(2,1)} reshape(bf16[16,8,10,1024]{3,2,1,0:T(8,128)(2,1)} %bitcast.35) | data formatting | bytes 5242880 | tf_op jit(solution)/shard_map/reshape | solution.py:62
  124.5 0.0 copy-done
  124.5 6.2 %convolution_convert_fusion = bf16[1280,1024]{1,0:T(8,128)(2,1)} fusion(bf16[1280,1024]{1,0:T(8,128)(2,1)} %reshape.46, bf16[1024,1024]{1,0:T(8,128)(2,1)S(1)} %copy-done), kind=kOutput, calls=%fused_computation.3 | convolution fusion | flops 2685665280 | bytes 7340032 | tf_op jit(solution)/shard_map/dot_general | solution.py:43
  130.6 0.0 copy-done.4
  130.7 0.0 copy-done.8
  130.7 3.1 convolution_convert_fusion.1
  133.8 0.0 copy-start.6
  133.8 0.0 copy-done.2
  133.8 0.8 fusion.4
  134.6 2.8 fusion.8
  137.4 0.0 copy-done.6
  137.4 3.4 convolution_convert_fusion.2
  140.8 2.6 multiply_reduce_fusion
  143.4 3.2 multiply_convert_fusion
  146.6 7.6 %convolution_bitcast_fusion.1 = f32[1024,1024]{0,1:T(8,128)} fusion(bf16[1280,1024]{1,0:T(8,128)(2,1)} %bitcast.40, bf16[1280,1024]{1,0:T(8,128)(2,1)} %reshape.46), kind=kOutput, calls=%fused_computation.6 | convolution fusion | flops 2684354560 | bytes 9437184 | tf_op jit(solution)/shard_map/dot_general | solution.py:51
  154.2 4.4 convolution_bitcast_fusion
  158.7 0.0 all-reduce.5.cloned.1.call-update
  158.7 0.0 all-reduce.7.cloned.1.call-start
  158.8 174.6 %all-reduce.5.cloned.1.call-done = (f32[1024,1024]{0,1:T(8,128)}, f32[1024,1024]{0,1:T(8,128)}) async-done(((f32[1024,1024]{0,1:T(8,128)}, f32[1024,1024]{0,1:T(8,128)}), (f32[1024,1024]{0,1:T(8,128)}, f32[1024,1024]{0,1:T(8,128)})) %all-reduce.5.cloned.1.call-update) | async-done | bytes 8388624 | tf_op jit(solution)/shard_map/psum | solution.py:68
  333.3 0.0 all-reduce.7.cloned.1.call-update
  333.4 3.8 convolution_convert_fusion.3
  337.2 172.1 %all-reduce.7.cloned.1.call-done = (f32[1024,1024]{0,1:T(8,128)}, f32[1024,1024]{0,1:T(8,128)}) async-done(((f32[1024,1024]{0,1:T(8,128)}, f32[1024,1024]{0,1:T(8,128)}), (f32[1024,1024]{0,1:T(8,128)}, f32[1024,1024]{0,1:T(8,128)})) %all-reduce.7.cloned.1.call-update) | async-done | bytes 8388624 | tf_op jit(solution)/shard_map/psum | solution.py:68
  509.3 5.3 %copy.16 = f32[1024,1024]{1,0:T(8,128)} copy(f32[1024,1024]{0,1:T(8,128)} %get-tuple-element.14) | data formatting | bytes 8388608
  514.6 5.5 %copy.17 = f32[1024,1024]{1,0:T(8,128)} copy(f32[1024,1024]{0,1:T(8,128)} %get-tuple-element.15) | data formatting | bytes 8388608
  (10 shorter events, 0.0 us)
Async XLA Ops:
  7.2 117.3 %copy-start = (bf16[1024,1024]{1,0:T(8,128)(2,1)S(1)}, bf16[1024,1024]{1,0:T(8,128)(2,1)}, u32[]{:S(2)}) copy-start(bf16[1024,1024]{1,0:T(8,128)(2,1)} %param.11) | copy-start | bytes 6291460
  12.7 6.5 %copy-start.7 = (s32[16]{0:T(128)S(1)}, s32[16]{0:T(128)}, u32[]{:S(2)}) copy-start(s32[16]{0:T(128)} %param.9) | copy-start | bytes 196
  12.7 100.6 %all-to-all-start = ((bf16[128,10,1024]{2,1,0:T(8,128)(2,1)}), bf16[128,10,1024]{2,1,0:T(8,128)(2,1)}, u32[]{:S(2)}, u32[]{:S(2)}) async-start(bf16[128,10,1024]{2,1,0:T(8,128)(2,1)} %copy.14), calls=%async_computation | async-start | bytes 8388608 | tf_op jit(solution)/shard_map/all_to_all | solution.py:61
  19.2 314.1 %all-reduce.5.cloned.1.call-start = ((), (), s32[]{:S(2)}) async-start(), calls=%async_computation.1 | async-start | bytes 16777216 | tf_op jit(solution)/shard_map/psum | solution.py:68
  124.5 6.2 %copy-start.4 = (bf16[1280,1024]{1,0:T(8,128)(2,1)S(1)}, bf16[1280,1024]{1,0:T(8,128)(2,1)}, u32[]{:S(2)}) copy-start(bf16[1280,1024]{1,0:T(8,128)(2,1)} %reshape.46) | copy-start | bytes 7864324
  124.5 6.2 %copy-start.8 = (bf16[1024,1024]{1,0:T(8,128)(2,1)S(1)}, bf16[1024,1024]{1,0:T(8,128)(2,1)}, u32[]{:S(2)}) copy-start(bf16[1024,1024]{1,0:T(8,128)(2,1)} %param.10) | copy-start | bytes 6291460
  130.7 3.1 copy-start.2
  133.8 3.6 copy-start.6
  146.6 7.6 %copy-start.3 = (bf16[16,80,1024]{2,1,0:T(8,128)(2,1)S(1)}, bf16[16,80,1024]{2,1,0:T(8,128)(2,1)}, u32[]{:S(2)}) copy-start(bf16[16,80,1024]{2,1,0:T(8,128)(2,1)} %convolution_convert_fusion.2) | copy-start | bytes 7864324
  146.6 7.6 %copy-start.5 = (bf16[1280,1024]{1,0:T(8,128)(2,1)S(1)}, bf16[1280,1024]{1,0:T(8,128)(2,1)}, u32[]{:S(2)}) copy-start(bf16[1280,1024]{1,0:T(8,128)(2,1)} %reshape.46) | copy-start | bytes 7864324
  158.7 350.6 %all-reduce.7.cloned.1.call-start = ((), (), s32[]{:S(2)}) async-start(), calls=%async_computation.2 | async-start | bytes 16777216 | tf_op jit(solution)/shard_map/psum | solution.py:68
  514.6 5.5 %copy-start.1 = (bf16[1024,1024]{1,0:T(8,128)(2,1)S(1)}, bf16[1024,1024]{1,0:T(8,128)(2,1)}, u32[]{:S(2)}) copy-start(bf16[1024,1024]{1,0:T(8,128)(2,1)} %param.11) | copy-start | bytes 6291460
Sparse Core Ops, SparseCore 0:
  158.8 174.4 all-reduce.4
  337.1 172.1 all-reduce.6
